TPU v7x, 32 devices: a whole 2x2x4 slice. The times are simulated.
32 devices in a mesh: fsdp: 8 (over z, y), dom: 4 (over x, core).
Axes of the slice: x: 2, y: 2, z: 4, core: 2. Of those that a mesh axis runs over, the one named last changes fastest.
Arguments:
- hidden_states: bfloat16 [256, 128, 768], P(('fsdp', 'dom')), may hold values from -40 to 40
- title_tokens: int32 [256, 128], P(('fsdp', 'dom')), may hold values from 0 to 30521, as said below
- query_key_value: bfloat16 [768, 2304], P('fsdp'), may hold values from -0.5 to 2.5
- output_weight: bfloat16 [768, 768], P('fsdp'), may hold values from -0.21875 to 0.21875
- up_weight: bfloat16 [768, 3072], P('fsdp'), may hold values from -0.21875 to 0.21875
- down_weight: bfloat16 [3072, 768], P('fsdp'), may hold values from -0.109375 to 0.109375
- attention_gain: float32 [768], replicated, may hold values from 0.25 to 1.75
- feedforward_gain: float32 [768], replicated, may hold values from 0.25 to 1.75
- encoded: bfloat16 [16384, 768], P(('fsdp', 'dom')), may hold values from -6 to 6
- send_rows: int32 [32, 32, 48], P(('fsdp', 'dom')), may hold values from 0 to 511
- send_count: int32 [32, 32], P(('fsdp', 'dom')), may hold values from 6 to 48, as said below
- arrival_nodes: int32 [32, 32, 48], P(('fsdp', 'dom')), may hold values from 0 to 511
- sage_weight: bfloat16 [2, 768, 1024], P(None, 'fsdp'), may hold values from -0.21875 to 0.21875
- node_gain: float32 [1024], replicated, may hold values from 0.25 to 1.75
Outputs:
- title_vectors: bfloat16 [256, 768], P(('fsdp', 'dom'))
- node_output: bfloat16 [16384, 1024], P(('fsdp', 'dom'))
Inputs may be any that keep to these rules, and one draw needn't show every extreme that they name: `title_tokens`: in each title the nonzero ids come first and zeros fill the rest; at least 16 ids of every title are nonzero. `send_count`: in every draw some device receives exactly 48 valid slots from every device.
All inputs are finite; a program needn't handle non-finite values.
Results may differ from a plain program's by a relative error of at most 0.0056.
Values may be sent and summed in bfloat16 or wider, within the bound.
A program may use at most 192 MiB of HBM per device.

v0:
```python
import math

import jax
import jax.numpy as jnp
from jax import lax
from jax.sharding import PartitionSpec as P

HEADS = 12
HEAD_DIM = 64


LN_EPSILON = 1e-12


def layer_norm(values, gain):
    center = values - jnp.mean(values, axis=-1, keepdims=True)
    spread = jnp.mean(center * center, axis=-1, keepdims=True)
    return center * lax.rsqrt(spread + LN_EPSILON) * gain


def encode_titles(
    hidden_states,
    title_tokens,
    query_key_value,
    output_weight,
    up_weight,
    down_weight,
    attention_gain,
    feedforward_gain,
):
    titles, seq_len, width = hidden_states.shape
    flat = hidden_states.reshape(titles * seq_len, width)
    live = title_tokens != 0
    full_project, full_output = (
        lax.all_gather(query_key_value, "fsdp", axis=0, tiled=True),
        lax.all_gather(output_weight, "fsdp", axis=0, tiled=True),
    )
    projected = jnp.dot(flat, full_project, preferred_element_type=jnp.float32).astype(jnp.bfloat16)
    projected = projected.reshape(titles, seq_len, 3, HEADS, HEAD_DIM)
    query_states = projected[:, :, 0]
    key_states = projected[:, :, 1]
    value_states = projected[:, :, 2]
    scores = jnp.einsum(
        "tihd,tjhd->thij", query_states, key_states, preferred_element_type=jnp.float32
    )
    scores = scores * (1.0 / math.sqrt(HEAD_DIM))
    scores = jnp.where(live[:, None, None, :], scores, -jnp.inf)
    highest = jnp.max(scores, axis=-1, keepdims=True)
    weights = jnp.exp(scores - highest)
    probs = (weights / jnp.sum(weights, axis=-1, keepdims=True)).astype(jnp.bfloat16)
    context = jnp.einsum("thij,tjhd->tihd", probs, value_states, preferred_element_type=jnp.float32)
    context = context.astype(jnp.bfloat16).reshape(titles * seq_len, width)
    mixed = jnp.dot(context, full_output, preferred_element_type=jnp.float32)
    attended = layer_norm(flat.astype(jnp.float32) + mixed, attention_gain).astype(jnp.bfloat16)
    attended = lax.optimization_barrier(attended)
    full_up, full_down = (
        lax.all_gather(up_weight, "fsdp", axis=0, tiled=True),
        lax.all_gather(down_weight, "fsdp", axis=0, tiled=True),
    )
    inner = jax.nn.gelu(
        jnp.dot(attended, full_up, preferred_element_type=jnp.float32), approximate=False
    )
    inner = inner.astype(jnp.bfloat16)
    lowered = jnp.dot(inner, full_down, preferred_element_type=jnp.float32)
    token_out = layer_norm(attended.astype(jnp.float32) + lowered, feedforward_gain).reshape(
        titles, seq_len, width
    )
    live_weight = live.astype(jnp.float32)
    pooled = jnp.sum(token_out * live_weight[:, :, None], axis=1) / jnp.sum(
        live_weight, axis=1, keepdims=True
    )
    return pooled.astype(jnp.bfloat16)


def scatter_sums(arrived, targets, valid, nodes):
    width = arrived.shape[2]
    mask_flat = valid.reshape(-1).astype(jnp.float32)
    label_flat = targets.reshape(-1)
    rows = arrived.reshape(-1, width).astype(jnp.float32) * mask_flat[:, None]
    sums = jax.ops.segment_sum(rows, label_flat, num_segments=nodes)
    degree = jax.ops.segment_sum(mask_flat, label_flat, num_segments=nodes)
    return (sums, degree)


def on_device(
    hidden_states,
    title_tokens,
    query_key_value,
    output_weight,
    up_weight,
    down_weight,
    attention_gain,
    feedforward_gain,
    encoded,
    send_rows,
    send_count,
    arrival_nodes,
    sage_weight,
    node_gain,
):
    titles = hidden_states.shape[0]
    nodes, width = encoded.shape
    outgoing = jnp.take(encoded, send_rows[0], axis=0)
    slot_count = outgoing.shape[1]
    counts_out = send_count[0].astype(jnp.bfloat16)
    arrived, arrived_counts = (
        lax.all_to_all(outgoing, ("fsdp", "dom"), split_axis=0, concat_axis=0, tiled=True),
        lax.all_to_all(counts_out, ("fsdp", "dom"), split_axis=0, concat_axis=0, tiled=True),
    )
    valid = (
        jnp.arange(slot_count, dtype=jnp.int32)[None, :] < arrived_counts.astype(jnp.int32)[:, None]
    )
    targets = arrival_nodes[0]
    title_vectors = encode_titles(
        hidden_states,
        title_tokens,
        query_key_value,
        output_weight,
        up_weight,
        down_weight,
        attention_gain,
        feedforward_gain,
    )
    sums, degree = scatter_sums(arrived, targets, valid, nodes)
    neighbour_mean = (sums / jnp.maximum(degree, 1.0)[:, None]).astype(jnp.bfloat16)
    self_rows = jnp.concatenate([title_vectors, encoded[titles:]], axis=0)
    piece = lax.all_gather(sage_weight, "fsdp", axis=1, tiled=True)
    running = jnp.dot(self_rows, piece[0], preferred_element_type=jnp.float32)
    combined = running + jnp.dot(neighbour_mean, piece[1], preferred_element_type=jnp.float32)
    node_output = layer_norm(combined, node_gain).astype(jnp.bfloat16)
    return (title_vectors, node_output)


def solution(mesh):
    return jax.shard_map(
        on_device,
        mesh=mesh,
        in_specs=(
            P(("fsdp", "dom"), None, None),
            P(("fsdp", "dom"), None),
            P("fsdp", None),
            P("fsdp", None),
            P("fsdp", None),
            P("fsdp", None),
            P(),
            P(),
            P(("fsdp", "dom"), None),
            P(("fsdp", "dom"), None, None),
            P(("fsdp", "dom"), None),
            P(("fsdp", "dom"), None, None),
            P(None, "fsdp", None),
            P(),
        ),
        out_specs=(P(("fsdp", "dom"), None), P(("fsdp", "dom"), None)),
        check_vma=False,
    )
```

profile of v0, /device:TPU:0, one launch (start us, length us, event | category | flops | bytes accessed | tf_op | source)
XLA Modules:
  0.0 387.5 jit_solution(11818364927257436339)
XLA Ops:
  7.2 0.7 all-gather.6.cloned.1.call-update
  8.0 0.7 all-gather.8.cloned.1.call-update
  8.7 0.7 all-gather.10.cloned.1.call-update
  10.6 0.7 copy.50
  11.3 7.3 %all-to-all-start.1 = ((bf16[32,1,1]{2,1,0:T(2,128)(2,1)}), bf16[32,1,1]{2,1,0:T(2,128)(2,1)S(1)}, u32[]{:S(2)}, u32[]{:S(2)}) async-start(bf16[32,1,1]{2,1,0:T(2,128)(2,1)} %copy.50), calls=%async_computation.1 | async-start | bytes 32768 | tf_op jit(solution)/shard_map/all_to_all | solution.py:108
  18.7 0.7 compare_select_fusion
  19.5 5.0 %gather_fusion = bf16[1536,768]{1,0:T(8,128)(2,1)S(1)} fusion(bf16[512,768]{1,0:T(8,128)(2,1)S(1)} %copy-done, s32[2048]{0:T(1024)S(1)} %pad_clamp_fusion), kind=kCustom, calls=%fused_computation | custom fusion | bytes 4724736 | tf_op jit(solution)/shard_map/jit(_take)/gather | solution.py:103
  24.5 1.7 broadcast_select_fusion
  26.2 5.8 %all-to-all-start = ((bf16[32,48,768]{2,1,0:T(8,128)(2,1)}), bf16[32,48,768]{2,1,0:T(8,128)(2,1)S(1)}, u32[]{:S(2)}, u32[]{:S(2)}) async-start(bf16[32,48,768]{2,1,0:T(8,128)(2,1)} %broadcast_select_fusion), calls=%async_computation | async-start | bytes 4718592 | tf_op jit(solution)/shard_map/all_to_all | solution.py:107
  32.7 2.6 copy.54
  35.5 0.7 convert_reduce_fusion
  36.3 11.1 %scatter_custom_fusion.1 = f32[512]{0:T(512)S(1)} fusion(s32[1536]{0:T(1024)S(1)} %reshape.151, f32[1536]{0:T(1024)S(1)} %reshape.161, f32[]{:T(128)} %constant.42.clone.1), kind=kCustom, calls=%fused_computation.81 | custom fusion | flops 1536 | bytes 2052 | tf_op jit(solution)/shard_map/scatter-add | solution.py:81
  47.5 70.7 %all-to-all-done = bf16[32,48,768]{2,1,0:T(8,128)(2,1)S(1)} async-done(((bf16[32,48,768]{2,1,0:T(8,128)(2,1)}), bf16[32,48,768]{2,1,0:T(8,128)(2,1)S(1)}, u32[]{:S(2)}, u32[]{:S(2)}) %all-to-all-start) | async-done | bytes 2359328 | tf_op jit(solution)/shard_map/all_to_all | solution.py:107
  118.2 12.7 %scatter_custom_fusion = f32[512,768]{1,0:T(8,128)} fusion(s32[1536]{0:T(1024)S(1)} %reshape.151, bf16[1536,768]{1,0:T(8,128)(2,1)S(1)} %bitcast.72, f32[1536]{0:T(1024)S(1)} %reshape.161, f32[]{:T(128)} %constant.42.clone.1), kind=kCustom, calls=%fused_computation.30 | custom fusion | flops 3538944 | bytes 3940356 | tf_op jit(solution)/shard_map/scatter-add | solution.py:80
  130.9 8.5 %convolution_convert_fusion = bf16[1024,2304]{1,0:T(8,128)(2,1)} fusion(bf16[1024,768]{1,0:T(8,128)(2,1)} %bitcast.74, bf16[768,2304]{1,0:T(8,128)(2,1)} %all-gather.6.cloned.1.call-done), kind=kOutput, calls=%fused_computation.27 | convolution fusion | flops 3626237952 | bytes 9830400 | tf_op jit(solution)/shard_map/dot_general | solution.py:38
  139.5 6.7 %copy.42 = bf16[1024,2304]{0,1:T(8,128)(2,1)} copy(bf16[1024,2304]{1,0:T(8,128)(2,1)} %convolution_convert_fusion) | data formatting | bytes 9437184 | tf_op jit(solution)/shard_map/convert_element_type | solution.py:38
  146.2 3.6 copy.58
  150.1 1.0 fusion.26
  151.2 2.6 fusion.70
  153.8 1.0 fusion.27
  154.8 1.2 copy.47
  156.1 2.8 fusion.71
  159.3 1.6 multiply_convert_fusion
  160.9 74.0 %all-gather.10.cloned.1.call-done = bf16[768,3072]{1,0:T(8,128)(2,1)} async-done(((bf16[96,3072]{1,0:T(8,128)(2,1)}), bf16[768,3072]{1,0:T(8,128)(2,1)}) %all-gather.10.cloned.1.call-update) | async-done | bytes 4718608 | tf_op jit(solution)/shard_map/all_gather | solution.py:57
  234.9 79.8 %all-gather.12.cloned.1.call-done = bf16[3072,768]{1,0:T(8,128)(2,1)} async-done(((bf16[384,768]{1,0:T(8,128)(2,1)}), bf16[3072,768]{1,0:T(8,128)(2,1)}) %all-gather.12.cloned.1.call-update) | async-done | bytes 4718608 | tf_op jit(solution)/shard_map/all_gather | solution.py:58
  314.7 39.7 %fusion.72 = (f32[1024]{0:T(1024)S(1)}, f32[1024,768]{0,1:T(8,128)S(1)}) fusion(bf16[3072,768]{1,0:T(8,128)(2,1)} %all-gather.12.cloned.1.call-done, bf16[1024,768]{0,1:T(8,128)(2,1)} %multiply_convert_fusion, bf16[768,3072]{1,0:T(8,128)(2,1)} %all-gather.10.cloned.1.call-done), kind=kOutput, calls=%fused_computation.120 | convolution fusion | flops 9870507008 | bytes 14159872 | tf_op jit(solution)/shard_map/dot_general | solution.py:64
  355.2 0.7 copy.60
  355.9 0.9 multiply_reduce_fusion
  357.0 18.1 %all-gather.14.cloned.1.call-done = bf16[2,768,1024]{2,1,0:T(8,128)(2,1)} async-done(((bf16[2,96,1024]{2,1,0:T(8,128)(2,1)}), bf16[2,768,1024]{2,1,0:T(8,128)(2,1)}) %all-gather.14.cloned.1.call-update) | async-done | bytes 3145744 | tf_op jit(solution)/shard_map/all_gather | solution.py:127
  375.1 2.5 fusion.25
  377.7 1.2 fusion.73
  379.2 1.3 multiply_convert_fusion.1
  (57 shorter events, 4.5 us)
Async XLA Ops:
  7.2 12.3 %copy-start = (bf16[512,768]{1,0:T(8,128)(2,1)S(1)}, bf16[512,768]{1,0:T(8,128)(2,1)}, u32[]{:S(2)}) copy-start(bf16[512,768]{1,0:T(8,128)(2,1)} %param.22) | copy-start | bytes 2359300
  7.2 123.7 %all-gather.6.cloned.1.call-start = ((), (), s32[]{:S(2)}) async-start(), calls=%async_computation.2 | async-start | bytes 3981312 | tf_op jit(solution)/shard_map/all_gather | solution.py:35
  7.9 148.2 %all-gather.8.cloned.1.call-start = ((), (), s32[]{:S(2)}) async-start(), calls=%async_computation.3 | async-start | bytes 1327104 | tf_op jit(solution)/shard_map/all_gather | solution.py:36
  8.7 226.2 %all-gather.10.cloned.1.call-start = ((), (), s32[]{:S(2)}) async-start(), calls=%async_computation.4 | async-start | bytes 5308416 | tf_op jit(solution)/shard_map/all_gather | solution.py:57
  9.4 305.3 %all-gather.12.cloned.1.call-start = ((), (), s32[]{:S(2)}) async-start(), calls=%async_computation.5 | async-start | bytes 5308416 | tf_op jit(solution)/shard_map/all_gather | solution.py:58
  11.3 14.9 %all-to-all-start.1 = ((bf16[32,1,1]{2,1,0:T(2,128)(2,1)}), bf16[32,1,1]{2,1,0:T(2,128)(2,1)S(1)}, u32[]{:S(2)}, u32[]{:S(2)}) async-start(bf16[32,1,1]{2,1,0:T(2,128)(2,1)} %copy.50), calls=%async_computation.1 | async-start | bytes 32768 | tf_op jit(solution)/shard_map/all_to_all | solution.py:108
  19.5 5.0 %copy-start.3 = (s32[1,32,48]{2,1,0:T(8,128)S(1)}, s32[1,32,48]{2,1,0:T(8,128)}, u32[]{:S(2)}) copy-start(s32[1,32,48]{2,1,0:T(8,128)} %param.23) | copy-start | bytes 18436
  26.2 92.0 %all-to-all-start = ((bf16[32,48,768]{2,1,0:T(8,128)(2,1)}), bf16[32,48,768]{2,1,0:T(8,128)(2,1)S(1)}, u32[]{:S(2)}, u32[]{:S(2)}) async-start(bf16[32,48,768]{2,1,0:T(8,128)(2,1)} %broadcast_select_fusion), calls=%async_computation | async-start | bytes 4718592 | tf_op jit(solution)/shard_map/all_to_all | solution.py:107
  32.1 3.2 copy-start.7
  32.1 3.3 copy-start.4
  32.1 343.0 %all-gather.14.cloned.1.call-start = ((), (), s32[]{:S(2)}) async-start(), calls=%async_computation.6 | async-start | bytes 3538944 | tf_op jit(solution)/shard_map/all_gather | solution.py:127
  153.8 2.3 copy-start.2
  156.1 3.2 copy-start.8
  160.9 193.9 %copy-start.9 = (f32[768]{0:T(1024)S(1)}, f32[768]{0:T(1024)}, u32[]{:S(2)}) copy-start(f32[768]{0:T(1024)} %param.21) | copy-start | bytes 9220
  355.9 19.2 %slice-start = ((bf16[512,768]{1,0:T(8,128)(2,1)}), bf16[504,768]{1,0:T(8,128)(2,1)S(1)}, s32[]{:S(2)}) async-start(bf16[512,768]{1,0:T(8,128)(2,1)} %param.22), calls=%async_computation.7 | async-start | bytes 1548288 | tf_op jit(solution)/shard_map/slice | solution.py:126
  356.8 20.8 %copy-start.1 = (f32[512,768]{1,0:T(8,128)S(1)}, f32[512,768]{1,0:T(8,128)}, u32[]{:S(2)}) copy-start(f32[512,768]{1,0:T(8,128)} %scatter_custom_fusion) | copy-start | bytes 4718596
  357.0 21.9 %copy-start.5 = (bf16[8,768]{1,0:T(8,128)(2,1)}, bf16[8,768]{1,0:T(8,128)(2,1)S(1)}, u32[]{:S(2)}) copy-start(bf16[8,768]{1,0:T(8,128)(2,1)S(1)} %copy.51) | copy-start | bytes 36868
  375.1 2.6 copy-start.10
  377.7 1.6 copy-start.6
Sparse Core Ops, SparseCore 0:
  10.2 103.0 all-gather.5
  115.4 39.1 all-gather.7
  156.9 78.0 all-gather.9
  236.9 77.6 all-gather.11
  316.7 58.3 all-gather.13
where the time goes:
time: 393 us; the launch traced here: 388 us
  waiting for transfers between devices  246 us (63%)
  matrix products  56.8 us (14%)
  other arithmetic  35.8 us (9%)
  local copies, waits for them, and re-layouts  21.3 us (5%)
  between operations  14.5 us (4%)
  starting transfers between devices  13.4 us (3%)
    all_gather x1, waiting for transfers between devices, encode_titles(): lax.all_gather(down_weight, 'fsdp', axis=0, tiled=True)  79.8 us
    all_gather x1, waiting for transfers between devices, encode_titles(): lax.all_gather(up_weight, 'fsdp', axis=0, tiled=True)  74 us
    all_to_all x1, waiting for transfers between devices, on_device(): lax.all_to_all(outgoing, ('fsdp', 'dom'), split_axis=0, concat_axis=0, ti...  70.7 us
    dot_general x1, matrix products, encode_titles(): lowered = jnp.dot(inner, full_down, preferred_element_type=jnp.float32)  39.7 us
    all_gather x1, waiting for transfers between devices, on_device(): piece = lax.all_gather(sage_weight, 'fsdp', axis=1, tiled=True)  18.1 us
    scatter-add x1, other arithmetic, scatter_sums(): sums = jax.ops.segment_sum(rows, label_flat, num_segments=nodes)  12.7 us
    scatter-add x1, other arithmetic, scatter_sums(): degree = jax.ops.segment_sum(mask_flat, label_flat, num_segments=nodes)  11.1 us
    dot_general x1, matrix products, encode_titles(): jnp.dot(flat, full_project, preferred_element_type=jnp.float32)  8.55 us
  transfers between devices with their start and end apart: 7, of which 4 were waited for; matrix products, arithmetic and copies ran while one was open for 28% of the time, Pallas kernels for 0%

commit v1 on v0

--- a/solution.py
+++ b/solution.py
@@ -1,9 +1,14 @@
+import functools
 import math
 
 import jax
 import jax.numpy as jnp
 from jax import lax
+from jax.experimental import pallas as pl
+from jax.experimental.pallas import tpu as pltpu
 from jax.sharding import PartitionSpec as P
+
+MESH = pl.DeviceIdType.MESH
 
 HEADS = 12
 HEAD_DIM = 64
@@ -18,23 +23,211 @@
     return center * lax.rsqrt(spread + LN_EPSILON) * gain
 
 
+def gather_kernel(outer, inner, arity, *refs):
+    shards, fulls = refs[:arity], refs[arity : 2 * arity]
+    (own_sem, outer_send, outer_recv, inner_send, inner_recv, pair_send, pair_recv, core_send, core_recv) = refs[2 * arity :]
+    me = lax.axis_index("fsdp")
+    spot = lax.axis_index("dom")
+    row, column = me // inner, lax.rem(me, inner)
+    base = (spot // 4) * 4
+    side = lax.rem(spot, 4) // 2
+    core = lax.rem(spot, 2)
+    pair_peer = base + (1 - side) * 2 + core
+    core_peer = base + side * 2 + (1 - core)
+    outer_peers = [lax.rem(row + step, outer) * inner + column for step in range(1, outer)]
+    inner_peers = [row * inner + lax.rem(column + step, inner) for step in range(1, inner)]
+
+    barrier = pltpu.get_barrier_semaphore()
+    for peer in outer_peers + inner_peers:
+        pl.semaphore_signal(barrier, inc=1, device_id=(peer, spot), device_id_type=MESH)
+    for peer in (pair_peer, core_peer):
+        pl.semaphore_signal(barrier, inc=1, device_id=(me, peer), device_id_type=MESH)
+    pl.semaphore_wait(barrier, outer + inner)
+
+    def part(ref, start, count):
+        if len(ref.shape) == 3:
+            return ref.at[:, pl.ds(start, count), :]
+        return ref.at[pl.ds(start, count), :]
+
+    def rows_of(which):
+        return shards[which].shape[-2]
+
+    def unit_of(which):
+        return rows_of(which) // 6
+
+    def block_start(which, back, over):
+        owner = lax.rem(row - back + outer, outer) * inner + lax.rem(column - over + inner, inner)
+        return pl.multiple_of(owner * rows_of(which), 8)
+
+    def own_copy(which):
+        return pltpu.make_async_copy(
+            shards[which],
+            part(fulls[which], block_start(which, 0, 0), rows_of(which)),
+            own_sem.at[which],
+        )
+
+    def outer_copy(which, step, receive=False):
+        unit = unit_of(which)
+        first = (3 * core + side) * unit
+        back = step if receive else 0
+        return pltpu.make_async_remote_copy(
+            src_ref=part(shards[which], pl.multiple_of(first, 8), 2 * unit),
+            dst_ref=part(fulls[which], pl.multiple_of(block_start(which, back, 0) + first, 8), 2 * unit),
+            send_sem=outer_send.at[which, step - 1],
+            recv_sem=outer_recv.at[which, step - 1],
+            device_id=(outer_peers[step - 1], spot),
+            device_id_type=MESH,
+        )
+
+    def inner_copy(which, back, over, receive=False):
+        unit = unit_of(which)
+        first = (3 * core + side) * unit
+        target = part(
+            fulls[which],
+            pl.multiple_of(block_start(which, back, over if receive else 0) + first, 8),
+            2 * unit,
+        )
+        if back == 0 and not receive:
+            source = part(shards[which], pl.multiple_of(first, 8), 2 * unit)
+        else:
+            source = target
+        return pltpu.make_async_remote_copy(
+            src_ref=source,
+            dst_ref=target,
+            send_sem=inner_send.at[which, back, over - 1],
+            recv_sem=inner_recv.at[which, back, over - 1],
+            device_id=(inner_peers[over - 1], spot),
+            device_id_type=MESH,
+        )
+
+    def pair_copy(which, back, over, receive=False):
+        unit = unit_of(which)
+        edge = 1 - side if receive else side
+        piece = part(
+            fulls[which],
+            pl.multiple_of(block_start(which, back, over) + (3 * core + 2 * edge) * unit, 8),
+            unit,
+        )
+        return pltpu.make_async_remote_copy(
+            src_ref=piece,
+            dst_ref=piece,
+            send_sem=pair_send.at[which, back, over],
+            recv_sem=pair_recv.at[which, back, over],
+            device_id=(me, pair_peer),
+            device_id_type=MESH,
+        )
+
+    def core_copy(which, back, over, receive=False):
+        unit = unit_of(which)
+        half = 1 - core if receive else core
+        piece = part(
+            fulls[which],
+            pl.multiple_of(block_start(which, back, over) + 3 * half * unit, 8),
+            3 * unit,
+        )
+        return pltpu.make_async_remote_copy(
+            src_ref=piece,
+            dst_ref=piece,
+            send_sem=core_send.at[which, back, over],
+            recv_sem=core_recv.at[which, back, over],
+            device_id=(me, core_peer),
+            device_id_type=MESH,
+        )
+
+    blocks = [(back, over) for over in range(inner) for back in range(outer) if (back, over) != (0, 0)]
+
+    for which in range(arity):
+        for step in range(outer - 1, 0, -1):
+            outer_copy(which, step).start()
+        for over in range(1, inner):
+            inner_copy(which, 0, over).start()
+        own_copy(which).start()
+
+    def outer_stage(which):
+        for step in range(1, outer):
+            outer_copy(which, step, receive=True).wait_recv()
+            for over in range(1, inner):
+                inner_copy(which, step, over).start()
+            pair_copy(which, step, 0).start()
+
+    def inner_stage(which):
+        for over in range(1, inner):
+            for back in range(outer):
+                inner_copy(which, back, over, receive=True).wait_recv()
+                pair_copy(which, back, over).start()
+
+    def pair_stage(which):
+        for back, over in blocks:
+            pair_copy(which, back, over, receive=True).wait_recv()
+            core_copy(which, back, over).start()
+
+    for tick in range(arity + 2):
+        if tick < arity:
+            outer_stage(tick)
+        if 0 <= tick - 1 < arity:
+            inner_stage(tick - 1)
+        if 0 <= tick - 2 < arity:
+            pair_stage(tick - 2)
+
+    for which in range(arity):
+        own_copy(which).wait()
+        for step in range(1, outer):
+            outer_copy(which, step).wait_send()
+        for over in range(1, inner):
+            for back in range(outer):
+                inner_copy(which, back, over).wait_send()
+        for back, over in blocks:
+            pair_copy(which, back, over).wait_send()
+            core_copy(which, back, over).wait_send()
+            core_copy(which, back, over, receive=True).wait_recv()
+
+
+def gather_weights(fsdp, *weights):
+    outer = 4 if fsdp % 4 == 0 else 1
+    inner = fsdp // outer
+    arity = len(weights)
+    shapes = []
+    for weight in weights:
+        shape = list(weight.shape)
+        shape[-2] *= fsdp
+        shapes.append(jax.ShapeDtypeStruct(tuple(shape), weight.dtype))
+    dma = pltpu.SemaphoreType.DMA
+    moved = sum(weight.size * weight.dtype.itemsize for weight in weights)
+    return pl.pallas_call(
+        functools.partial(gather_kernel, outer, inner, arity),
+        out_shape=tuple(shapes),
+        in_specs=[pl.BlockSpec(memory_space=pltpu.VMEM)] * arity,
+        out_specs=tuple([pl.BlockSpec(memory_space=pl.ANY)] * arity),
+        scratch_shapes=[
+            dma((arity,)),
+            dma((arity, outer - 1)),
+            dma((arity, outer - 1)),
+            dma((arity, outer, inner - 1)),
+            dma((arity, outer, inner - 1)),
+            dma((arity, outer, inner)),
+            dma((arity, outer, inner)),
+            dma((arity, outer, inner)),
+            dma((arity, outer, inner)),
+        ],
+        compiler_params=pltpu.CompilerParams(collective_id=0, has_side_effects=True),
+        cost_estimate=pl.CostEstimate(flops=60_000_000_000, bytes_accessed=moved * fsdp, transcendentals=0),
+        name="gather_weights",
+    )(*weights)
+
+
 def encode_titles(
     hidden_states,
     title_tokens,
-    query_key_value,
-    output_weight,
-    up_weight,
-    down_weight,
+    full_project,
+    full_output,
+    full_up,
+    full_down,
     attention_gain,
     feedforward_gain,
 ):
     titles, seq_len, width = hidden_states.shape
     flat = hidden_states.reshape(titles * seq_len, width)
     live = title_tokens != 0
-    full_project, full_output = (
-        lax.all_gather(query_key_value, "fsdp", axis=0, tiled=True),
-        lax.all_gather(output_weight, "fsdp", axis=0, tiled=True),
-    )
     projected = jnp.dot(flat, full_project, preferred_element_type=jnp.float32).astype(jnp.bfloat16)
     projected = projected.reshape(titles, seq_len, 3, HEADS, HEAD_DIM)
     query_states = projected[:, :, 0]
@@ -53,10 +246,6 @@
     mixed = jnp.dot(context, full_output, preferred_element_type=jnp.float32)
     attended = layer_norm(flat.astype(jnp.float32) + mixed, attention_gain).astype(jnp.bfloat16)
     attended = lax.optimization_barrier(attended)
-    full_up, full_down = (
-        lax.all_gather(up_weight, "fsdp", axis=0, tiled=True),
-        lax.all_gather(down_weight, "fsdp", axis=0, tiled=True),
-    )
     inner = jax.nn.gelu(
         jnp.dot(attended, full_up, preferred_element_type=jnp.float32), approximate=False
     )
@@ -83,6 +272,7 @@
 
 
 def on_device(
+    fsdp,
     hidden_states,
     title_tokens,
     query_key_value,
@@ -111,20 +301,22 @@
         jnp.arange(slot_count, dtype=jnp.int32)[None, :] < arrived_counts.astype(jnp.int32)[:, None]
     )
     targets = arrival_nodes[0]
+    full_project, full_output, full_up, full_down, piece = gather_weights(
+        fsdp, query_key_value, output_weight, up_weight, down_weight, sage_weight
+    )
     title_vectors = encode_titles(
         hidden_states,
         title_tokens,
-        query_key_value,
-        output_weight,
-        up_weight,
-        down_weight,
+        full_project,
+        full_output,
+        full_up,
+        full_down,
         attention_gain,
         feedforward_gain,
     )
     sums, degree = scatter_sums(arrived, targets, valid, nodes)
     neighbour_mean = (sums / jnp.maximum(degree, 1.0)[:, None]).astype(jnp.bfloat16)
     self_rows = jnp.concatenate([title_vectors, encoded[titles:]], axis=0)
-    piece = lax.all_gather(sage_weight, "fsdp", axis=1, tiled=True)
     running = jnp.dot(self_rows, piece[0], preferred_element_type=jnp.float32)
     combined = running + jnp.dot(neighbour_mean, piece[1], preferred_element_type=jnp.float32)
     node_output = layer_norm(combined, node_gain).astype(jnp.bfloat16)
@@ -133,7 +325,7 @@
 
 def solution(mesh):
     return jax.shard_map(
-        on_device,
+        functools.partial(on_device, mesh.shape["fsdp"]),
         mesh=mesh,
         in_specs=(
             P(("fsdp", "dom"), None, None),

time: 393 us -> 240 us (0.61)
  waiting for transfers between devices: 246 us -> 0.01 us
  Pallas kernels: 0 us -> 99.2 us
  between operations: 14.5 us -> 1.3 us
  matrix products: 56.8 us -> 69.9 us
  local copies, waits for them, and re-layouts: 21.3 us -> 13.7 us
  other arithmetic: 35.8 us -> 40.3 us
    all_gather x5 -> x0, waiting for transfers between devices: 172 us -> none  [the longest x1 79.8 us: encode_titles(): lax.all_gather(down_weight, 'fsdp', axis=0, tiled=True)]
    pallas_call x0 -> x1, Pallas kernels: none -> 99.2 us  [gather_weights(): pl.pallas_call(functools.partial(gather_kernel, outer, inner, arity), out...]
    all_to_all x1, waiting for transfers between devices: 70.7 us -> 0.01 us  [on_device(): lax.all_to_all(outgoing, ('fsdp', 'dom'), split_axis=0, concat_axis=0, ti...]
    dot_general x1, matrix products: 39.7 us -> 52.7 us  [encode_titles(): lowered = jnp.dot(inner, full_down, preferred_element_type=jnp.float32)]
    convert_element_type x1 -> x0, local copies, waits for them, and re-layouts: 6.71 us -> none  [encode_titles(): jnp.dot(flat, full_project, preferred_element_type=jnp.float32)]
  transfers between devices with their start and end apart: 7 -> 2, of which waited for: 4 -> 0; matrix products, arithmetic and copies ran while one was open for 28% -> 43% of each run, Pallas kernels for 0% -> 42%
where the time goes in v1:
time: 240 us; the launch traced here: 237 us
  Pallas kernels  99.2 us (41%)
  matrix products  69.9 us (29%)
  other arithmetic  40.3 us (17%)
  local copies, waits for them, and re-layouts  13.7 us (6%)
  starting transfers between devices  12.2 us (5%)
    pallas_call x1, Pallas kernels, gather_weights(): pl.pallas_call(functools.partial(gather_kernel, outer, inner, arity), out...  99.2 us
    dot_general x1, matrix products, encode_titles(): lowered = jnp.dot(inner, full_down, preferred_element_type=jnp.float32)  52.7 us
    scatter-add x1, other arithmetic, scatter_sums(): sums = jax.ops.segment_sum(rows, label_flat, num_segments=nodes)  12.5 us
    scatter-add x1, other arithmetic, scatter_sums(): degree = jax.ops.segment_sum(mask_flat, label_flat, num_segments=nodes)  11.1 us
    all_to_all x1, starting transfers between devices, on_device(): lax.all_to_all(counts_out, ('fsdp', 'dom'), split_axis=0, concat_axis=0,...  7.33 us
    dot_general x1, matrix products, encode_titles(): jnp.dot(flat, full_project, preferred_element_type=jnp.float32)  6.14 us
    gather x1, local copies, waits for them, and re-layouts, on_device(): outgoing = jnp.take(encoded, send_rows[0], axis=0)  4.97 us
    all_to_all x1, starting transfers between devices, on_device(): lax.all_to_all(outgoing, ('fsdp', 'dom'), split_axis=0, concat_axis=0, ti...  4.87 us
  transfers between devices with their start and end apart: 2, of which 0 were waited for; matrix products, arithmetic and copies ran while one was open for 43% of the time, Pallas kernels for 42%

profile of v1, /device:TPU:0, one launch (start us, length us, event | category | flops | bytes accessed | tf_op | source)
XLA Modules:
  0.0 236.6 jit_solution(17518744490935073027)
XLA Ops:
  0.6 0.7 convert_bitcast_fusion
  1.3 0.7 copy.47
  2.0 7.3 %all-to-all-start.1 = ((bf16[32,1,1]{2,1,0:T(2,128)(2,1)}), bf16[32,1,1]{2,1,0:T(2,128)(2,1)S(1)}, u32[]{:S(2)}, u32[]{:S(2)}) async-start(bf16[32,1,1]{2,1,0:T(2,128)(2,1)} %copy.47), calls=%async_computation.1 | async-start | bytes 32768 | tf_op jit(solution)/shard_map/all_to_all | solution.py:298
  9.3 0.7 compare_select_fusion
  10.1 0.7 compare_and_fusion
  10.8 1.7 copy.51
  12.5 99.2 %gather_weights.1 = (bf16[768,2304]{1,0:T(8,128)(2,1)}, bf16[768,768]{1,0:T(8,128)(2,1)}, bf16[768,3072]{1,0:T(8,128)(2,1)}, bf16[3072,768]{1,0:T(8,128)(2,1)}, bf16[2,768,1024]{2,1,0:T(8,128)(2,1)}) custom-call(bf16[96,2304]{1,0:T(8,128)(2,1)} %refs_0_.1, bf16[96,768]{1,0:T(8,128)(2,1)} %refs_1_.1, bf16[96,3072]{1,0:T(8,128)(2,1)} %refs_2_.1, ...), custom_call_target="tpu_custom_call" | custom-call | flops 60000002048 | bytes 17301504 | tf_op jit(solution)/shard_map/gather_weights/pallas_call | solution.py:196
  111.8 6.1 %fusion.20 = bf16[288,8,8,128]{3,1,2,0:T(8,128)(2,1)S(1)} fusion(bf16[768,2304]{1,0:T(8,128)(2,1)} %get-tuple-element.7, bf16[1024,768]{1,0:T(8,128)(2,1)S(1)} %bitcast.75), kind=kOutput, calls=%fused_computation.44 | convolution fusion | flops 3626237952 | bytes 9830400 | tf_op jit(solution)/shard_map/dot_general | solution.py:231
  117.9 1.2 copy.55
  120.0 1.0 fusion.26
  121.0 2.6 %fusion.75 = (f32[8,12,128]{2,1,0:T(8,128)S(1)}, f32[8,12,128,128]{2,3,1,0:T(8,128)S(1)}) fusion(f32[8,12,128,128]{2,3,1,0:T(8,128)S(1)} %fusion.26, pred[8,128]{1,0:T(8,128)(4,1)S(1)} %get-tuple-element.17), kind=kOutput, calls=%fused_computation.121 | output fusion | flops 9437311 | bytes 12633088 | tf_op jit(solution)/shard_map/sub | solution.py:242
  123.7 1.0 fusion.32
  124.6 1.2 copy.44
  125.9 1.6 fusion.76
  127.5 1.6 copy-done.1
  129.1 0.4 multiply_reduce_fusion.2
  129.6 3.4 %multiply_convert_fusion = bf16[1024,768]{0,1:T(8,128)(2,1)} fusion(f32[1024,768]{0,1:T(8,128)} %copy-done.1, f32[768]{0:T(1024)S(1)} %copy-done.8, f32[1024]{0:T(1024)S(1)} %add_rsqrt_fusion.1, f32[1024]{0:T(1024)S(1)} %broadcast_multiply_fusion.1), kind=kLoop, calls=%fused_computation.35 | loop fusion | flops 3145728 | bytes 4729856 | tf_op jit(solution)/shard_map/convert_element_type | solution.py:247
  133.1 5.0 %gather_fusion = bf16[1536,768]{1,0:T(8,128)(2,1)S(1)} fusion(bf16[512,768]{1,0:T(8,128)(2,1)S(1)} %copy-done, s32[2048]{0:T(1024)S(1)} %pad_clamp_fusion), kind=kCustom, calls=%fused_computation | custom fusion | bytes 4724736 | tf_op jit(solution)/shard_map/jit(_take)/gather | solution.py:293
  138.0 1.7 broadcast_select_fusion
  139.8 4.9 %all-to-all-start = ((bf16[32,48,768]{2,1,0:T(8,128)(2,1)}), bf16[32,48,768]{2,1,0:T(8,128)(2,1)S(1)}, u32[]{:S(2)}, u32[]{:S(2)}) async-start(bf16[32,48,768]{2,1,0:T(8,128)(2,1)} %broadcast_select_fusion), calls=%async_computation | async-start | bytes 4718592 | tf_op jit(solution)/shard_map/all_to_all | solution.py:297
  144.7 52.7 %fusion.77 = (f32[1024]{0:T(1024)S(1)}, f32[1024,768]{0,1:T(8,128)}) fusion(bf16[3072,768]{1,0:T(8,128)(2,1)} %get-tuple-element.10, bf16[1024,768]{0,1:T(8,128)(2,1)} %multiply_convert_fusion, bf16[768,3072]{1,0:T(8,128)(2,1)} %get-tuple-element.9), kind=kOutput, calls=%fused_computation.123 | convolution fusion | flops 9870507008 | bytes 14159872 | tf_op jit(solution)/shard_map/dot_general | solution.py:253
  197.4 2.4 %multiply_reduce_fusion.1 = f32[1024]{0:T(1024)S(1)} fusion(f32[1024,768]{0,1:T(8,128)} %get-tuple-element.26, f32[1024]{0:T(1024)S(1)} %broadcast_multiply_fusion), kind=kLoop, calls=%fused_computation.33 | loop fusion | flops 2358272 | bytes 3153920 | tf_op jit(solution)/shard_map/reduce_sum | solution.py:22
  199.8 0.4 copy-done.2
  200.2 0.4 multiply_bitcast_fusion
  200.6 0.7 copy.57
  201.4 0.9 multiply_reduce_fusion
  202.5 3.8 %fusion.28 = f32[512,1024]{1,0:T(8,128)} fusion(bf16[2,768,1024]{2,1,0:T(8,128)(2,1)} %get-tuple-element.11, bf16[504,768]{1,0:T(8,128)(2,1)S(1)} %slice-done, bf16[8,768]{1,0:T(8,128)(2,1)S(1)} %copy.48), kind=kOutput, calls=%fused_computation.56 | convolution fusion | flops 806879232 | bytes 4456448 | tf_op jit(solution)/shard_map/dot_general | solution.py:320
  206.3 0.7 convert_reduce_fusion
  207.1 11.1 %scatter_custom_fusion.1 = f32[512]{0:T(512)S(1)} fusion(s32[1536]{0:T(1024)S(1)} %reshape.151, f32[1536]{0:T(1024)S(1)} %reshape.161, f32[]{:T(128)} %constant.42.clone.1), kind=kCustom, calls=%fused_computation.84 | custom fusion | flops 1536 | bytes 2052 | tf_op jit(solution)/shard_map/scatter-add | solution.py:270
  218.3 12.5 %scatter_custom_fusion = f32[512,768]{1,0:T(8,128)} fusion(s32[1536]{0:T(1024)S(1)} %reshape.151, bf16[1536,768]{1,0:T(8,128)(2,1)S(1)} %bitcast.73, f32[1536]{0:T(1024)S(1)} %reshape.161, f32[]{:T(128)} %constant.42.clone.1), kind=kCustom, calls=%fused_computation.30 | custom fusion | flops 3538944 | bytes 3940356 | tf_op jit(solution)/shard_map/scatter-add | solution.py:269
  230.8 3.7 %fusion.78 = (f32[512]{0:T(512)S(1)}, f32[512,1024]{1,0:T(8,128)S(1)}) fusion(f32[512,1024]{1,0:T(8,128)} %fusion.28, bf16[2,768,1024]{2,1,0:T(8,128)(2,1)} %get-tuple-element.11, f32[512,768]{1,0:T(8,128)} %scatter_custom_fusion, f32[512]{0:T(512)S(1)} %broadcast_maximum_fusion), kind=kOutput, calls=%fused_computation.124 | convolution fusion | flops 807140864 | bytes 7344128 | tf_op jit(solution)/shard_map/dot_general | solution.py:321
  234.9 1.3 multiply_convert_fusion.1
  (42 shorter events, 1.7 us)
Async XLA Ops:
  2.0 137.8 %all-to-all-start.1 = ((bf16[32,1,1]{2,1,0:T(2,128)(2,1)}), bf16[32,1,1]{2,1,0:T(2,128)(2,1)S(1)}, u32[]{:S(2)}, u32[]{:S(2)}) async-start(bf16[32,1,1]{2,1,0:T(2,128)(2,1)} %copy.47), calls=%async_computation.1 | async-start | bytes 32768 | tf_op jit(solution)/shard_map/all_to_all | solution.py:298
  12.5 99.3 %copy-start.3 = (bf16[8,128,768]{2,1,0:T(8,128)(2,1)S(1)}, bf16[8,128,768]{2,1,0:T(8,128)(2,1)}, u32[]{:S(2)}) copy-start(bf16[8,128,768]{2,1,0:T(8,128)(2,1)} %param.14) | copy-start | bytes 4718596
  119.2 0.7 copy-start.7
  123.7 2.2 copy-start.10
  125.9 3.7 %copy-start.8 = (f32[768]{0:T(1024)S(1)}, f32[768]{0:T(1024)}, u32[]{:S(2)}) copy-start(f32[768]{0:T(1024)} %param.20) | copy-start | bytes 9220
  127.5 1.7 copy-start.1
  129.1 3.9 %copy-start = (bf16[512,768]{1,0:T(8,128)(2,1)S(1)}, bf16[512,768]{1,0:T(8,128)(2,1)}, u32[]{:S(2)}) copy-start(bf16[512,768]{1,0:T(8,128)(2,1)} %param.22) | copy-start | bytes 2359300
  139.8 78.5 %all-to-all-start = ((bf16[32,48,768]{2,1,0:T(8,128)(2,1)}), bf16[32,48,768]{2,1,0:T(8,128)(2,1)S(1)}, u32[]{:S(2)}, u32[]{:S(2)}) async-start(bf16[32,48,768]{2,1,0:T(8,128)(2,1)} %broadcast_select_fusion), calls=%async_computation | async-start | bytes 4718592 | tf_op jit(solution)/shard_map/all_to_all | solution.py:297
  197.4 2.8 %copy-start.2 = (f32[1024,768]{0,1:T(8,128)S(1)}, f32[1024,768]{0,1:T(8,128)}, u32[]{:S(2)}) copy-start(f32[1024,768]{0,1:T(8,128)} %get-tuple-element.26) | copy-start | bytes 9437188
  197.4 2.8 %copy-start.9 = (f32[768]{0:T(1024)S(1)}, f32[768]{0:T(1024)}, u32[]{:S(2)}) copy-start(f32[768]{0:T(1024)} %param.21) | copy-start | bytes 9220
  201.4 1.1 copy-start.4
  201.4 1.1 slice-start
  202.4 28.4 %copy-start.5 = (bf16[8,768]{1,0:T(8,128)(2,1)}, bf16[8,768]{1,0:T(8,128)(2,1)S(1)}, u32[]{:S(2)}) copy-start(bf16[8,768]{1,0:T(8,128)(2,1)S(1)} %copy.48) | copy-start | bytes 36868
  230.8 4.0 %copy-start.6 = (f32[1024]{0:T(1024)S(1)}, f32[1024]{0:T(1024)}, u32[]{:S(2)}) copy-start(f32[1024]{0:T(1024)} %param.27) | copy-start | bytes 12292
